TPU v7x, 8 devices: a whole 2x2x1 slice. The times are simulated.
8 devices in a mesh: dp: 2 (over z, y), tp: 4 (over x, core).
Axes of the slice: x: 2, y: 2, z: 1, core: 2. Of those that a mesh axis runs over, the one named last changes fastest.
Arguments:
- hidden_in: bfloat16 [256, 3072], P(('dp', 'tp')), parts along dimension 0
- attn_norm: bfloat16 [3072], replicated
- mlp_norm: bfloat16 [3072], replicated
- w_query: bfloat16 [3072, 24, 128], P(None, 'tp')
- w_key: bfloat16 [3072, 8, 128], replicated
- w_value: bfloat16 [3072, 8, 128], replicated
- w_out: bfloat16 [24, 128, 3072], P('tp')
- w_gate: bfloat16 [3072, 8192], P(None, 'tp')
- w_up: bfloat16 [3072, 8192], P(None, 'tp')
- w_down: bfloat16 [8192, 3072], P('tp')
Outputs:
- output 1: bfloat16 [256, 3072], P(('dp', 'tp')), parts along dimension 0
- output 2: bfloat16 [256, 8, 128], P('dp', 'tp'), parts along dimension 0
- output 3: bfloat16 [256, 8, 128], P('dp', 'tp'), parts along dimension 0
There are 2 independent parts. A program takes and returns all parts, laid end to end along the dimension named above; an argument that names none is the same for every part.
All inputs are finite; a program needn't handle non-finite values.
Results may differ from a plain program's by a relative error of at most 0.0144904.
Values are sent between devices in bfloat16 or wider.
A program may use at most 1 GiB of HBM per device.

v0:
```python
import jax
import jax.numpy as jnp
from jax import lax
from jax.sharding import PartitionSpec as P


def rms_norm(rows_in, gain_vec):
    rows_f = rows_in.astype(jnp.float32)
    mean_sq = jnp.mean(rows_f * rows_f, axis=-1, keepdims=True)
    return (rows_f * lax.rsqrt(mean_sq + 1e-5) * gain_vec.astype(jnp.float32)).astype(jnp.bfloat16)


def apply_rope(heads_f, positions):
    head_dim = heads_f.shape[-1]
    half_dim = head_dim // 2
    inv_freq = 1.0 / (500000.0 ** (jnp.arange(half_dim).astype(jnp.float32) * (2.0 / head_dim)))
    angles = positions[:, None] * inv_freq[None, :]
    cosine = jnp.cos(angles)[:, None, :]
    sine_val = jnp.sin(angles)[:, None, :]
    first_half = heads_f[..., :half_dim]
    second_half = heads_f[..., half_dim:]
    return jnp.concatenate([first_half * cosine - second_half * sine_val, second_half * cosine + first_half * sine_val], axis=-1)


def causal_attention(q_rot, k_rot, v_local):
    tokens = q_rot.shape[0]
    head_dim = q_rot.shape[-1]
    n_split = 8
    block_len = tokens // n_split
    pieces = []
    for block_idx in range(n_split):
        key_stop = (block_idx + 1) * block_len
        q_block = q_rot[block_idx * block_len:key_stop]
        scores = jnp.einsum("qgrd,kgd->grqk", q_block, k_rot[:key_stop], preferred_element_type=jnp.float32) * (head_dim ** -0.5)
        query_pos = block_idx * block_len + jnp.arange(block_len)
        visible = jnp.arange(key_stop)[None, :] <= query_pos[:, None]
        scores = jnp.where(visible, scores, -1e30)
        probs_bf = jax.nn.softmax(scores, axis=-1).astype(jnp.bfloat16)
        block_out = jnp.einsum("grqk,kgd->qgrd", probs_bf, v_local[:key_stop], preferred_element_type=jnp.float32)
        pieces.append(block_out.astype(jnp.bfloat16))
    return jnp.concatenate(pieces, axis=0)


def solution(mesh):
    tp_size = mesh.shape["tp"]

    def local_layer(hidden_in, attn_norm, mlp_norm, w_query, w_key, w_value, w_out, w_gate, w_up, w_down):
        kv_heads = w_key.shape[1]
        local_heads = w_query.shape[1]
        head_dim = w_query.shape[2]
        kv_local = max(kv_heads // tp_size, 1)
        first_kv = (lax.axis_index("tp") * kv_heads) // tp_size
        key_local = lax.dynamic_slice_in_dim(w_key, first_kv, kv_local, axis=1)
        value_local = lax.dynamic_slice_in_dim(w_value, first_kv, kv_local, axis=1)
        normed = rms_norm(hidden_in, attn_norm)
        gathered = lax.all_gather(normed, "tp", axis=0, tiled=True)
        tokens = gathered.shape[0]
        positions = jnp.arange(tokens).astype(jnp.float32)
        q_proj = jnp.einsum("td,dhe->the", gathered, w_query, preferred_element_type=jnp.float32)
        k_proj = jnp.einsum("td,dge->tge", gathered, key_local, preferred_element_type=jnp.float32)
        v_local = jnp.einsum("td,dge->tge", gathered, value_local, preferred_element_type=jnp.float32).astype(jnp.bfloat16)
        q_rot = apply_rope(q_proj, positions).astype(jnp.bfloat16).reshape(tokens, kv_local, local_heads // kv_local, head_dim)
        k_rot = apply_rope(k_proj, positions).astype(jnp.bfloat16)
        attn_out = causal_attention(q_rot, k_rot, v_local).reshape(tokens, local_heads, head_dim)
        attn_part = jnp.einsum("the,hed->td", attn_out, w_out, preferred_element_type=jnp.float32).astype(jnp.bfloat16)
        attn_sum = lax.psum_scatter(attn_part, "tp", scatter_dimension=0, tiled=True)
        resid_mid = (hidden_in.astype(jnp.float32) + attn_sum.astype(jnp.float32)).astype(jnp.bfloat16)
        normed_mlp = rms_norm(resid_mid, mlp_norm)
        gathered_mlp = lax.all_gather(normed_mlp, "tp", axis=0, tiled=True)
        gate_proj = jnp.dot(gathered_mlp, w_gate, preferred_element_type=jnp.float32)
        up_proj = jnp.dot(gathered_mlp, w_up, preferred_element_type=jnp.float32)
        mlp_act = (jax.nn.silu(gate_proj) * up_proj).astype(jnp.bfloat16)
        mlp_part = jnp.dot(mlp_act, w_down, preferred_element_type=jnp.float32).astype(jnp.bfloat16)
        mlp_sum = lax.psum_scatter(mlp_part, "tp", scatter_dimension=0, tiled=True)
        hidden_out = (resid_mid.astype(jnp.float32) + mlp_sum.astype(jnp.float32)).astype(jnp.bfloat16)
        return hidden_out, k_rot, v_local

    row_spec = P(("dp", "tp"), None)
    cache_spec = P("dp", "tp", None)
    return jax.shard_map(local_layer, mesh=mesh, in_specs=(row_spec, P(), P(), P(None, "tp", None), P(), P(), P("tp", None, None), P(None, "tp"), P(None, "tp"), P("tp", None)), out_specs=(row_spec, cache_spec, cache_spec), check_vma=False)
```

profile of v0, /device:TPU:0, one launch (start us, length us, event | category | flops | bytes accessed | tf_op | source)
XLA Modules:
  0.0 135.8 jit_solution(1574455769910430292)
XLA Ops:
  7.2 0.0 reduce-scatter.3.cloned.1.call-start
  7.3 0.7 convert_element_type.162
  8.0 1.1 fusion.65
  9.1 1.1 fusion.67
  10.2 13.0 %all_gather.6 = bf16[128,3072]{1,0:T(8,128)(2,1)S(1)} all-gather(bf16[32,3072]{1,0:T(8,128)(2,1)S(1)} %fusion.67), channel_id=1, replica_groups=mesh['dp'=2,'tp'=4] {'tp'}, dimensions={0}, use_global_device_ids=true | all-gather | bytes 983040 | tf_op jit(solution)/shard_map/all_gather | solution.py:56
  23.2 6.6 %copy.15 = bf16[3072,6,128]{0,2,1:T(8,128)(2,1)} copy(bf16[3072,6,128]{2,0,1:T(8,128)(2,1)} %param.13) | data formatting | bytes 9437184 | tf_op args[3]
  29.8 5.5 %constant_dynamic-slice_fusion = bf16[3072,2,128]{2,1,0:T(2,128)(2,1)} fusion(bf16[3072,8,128]{2,1,0:T(8,128)(2,1)} %param.14, s32[]{:T(128)S(6)} %select_n.42), kind=kLoop, calls=%fused_computation.204 | loop fusion | bytes 3145732 | tf_op jit(solution)/shard_map/dynamic_slice | solution.py:53
  35.3 3.6 %copy.77 = bf16[3072,2,128]{0,2,1:T(8,128)(2,1)S(1)} copy(bf16[3072,2,128]{2,1,0:T(2,128)(2,1)} %constant_dynamic-slice_fusion) | data formatting | bytes 3145728
  38.9 3.7 %fusion.136 = f32[128,768]{0,1:S(1)} fusion(bf16[128,3072]{1,0:T(8,128)(2,1)S(1)} %all_gather.6, bf16[3072,768]{0,1:T(8,128)(2,1)} %bitcast.199), kind=kOutput, calls=%fused_computation.224 | convolution fusion | flops 603979776 | bytes 5898240
  42.6 0.6 fusion.135
  43.2 0.2 multiply_cosine_fusion
  43.4 0.1 add_convert_fusion
  43.5 0.4 pad_maximum_fusion
  43.9 0.2 fusion.39
  44.2 4.3 %constant_dynamic-slice_fusion.1 = bf16[3072,2,128]{2,1,0:T(2,128)(2,1)S(1)} fusion(bf16[3072,8,128]{2,1,0:T(8,128)(2,1)} %param.15, s32[]{:T(128)S(6)} %select_n.42), kind=kLoop, calls=%fused_computation.205 | loop fusion | bytes 3145732 | tf_op jit(solution)/shard_map/dynamic_slice | solution.py:54
  48.5 0.4 fusion.12
  48.9 0.1 iota_compare_fusion.6
  49.0 0.2 fusion.40
  49.2 0.2 fusion.128
  49.4 0.1 iota_compare_fusion.5
  49.5 0.2 fusion.41
  49.7 0.2 fusion.129
  49.9 0.1 iota_compare_fusion.4
  49.9 0.2 fusion.42
  50.2 0.2 fusion.130
  50.4 0.1 iota_compare_fusion.3
  50.4 0.2 fusion.43
  50.6 0.2 fusion.131
  50.8 0.1 iota_compare_fusion.2
  50.9 0.2 fusion.44
  51.1 0.2 fusion.132
  51.3 0.1 iota_compare_fusion.1
  51.4 0.2 fusion.45
  51.6 0.2 fusion.133
  51.8 0.1 iota_compare_fusion
  51.9 0.2 fusion.46
  52.1 0.2 fusion.134
  52.3 0.2 fusion.48
  52.5 0.2 fusion.50
  52.8 0.2 fusion.52
  53.0 0.2 fusion.54
  53.2 0.2 fusion.56
  53.5 0.2 fusion.58
  53.7 0.2 fusion.60
  53.9 0.2 fusion.62
  54.2 0.0 copy-start.2
  54.2 0.0 copy-start
  54.2 4.0 %fusion.8 = bf16[128,3072]{1,0:T(8,128)(2,1)} fusion(bf16[128,6,128]{2,0,1:T(8,128)(2,1)S(1)} %bitcast.210, bf16[6,128,3072]{2,1,0:T(8,128)(2,1)} %param.16), kind=kOutput, calls=%fused_computation.9 | convolution fusion | flops 604372992 | bytes 5701632 | tf_op jit(solution)/shard_map/the,hed->td/dot_general | solution.py:65
  58.2 0.0 reduce-scatter.3.cloned.1.call-update
  58.3 0.0 reduce-scatter.5.cloned.1.call-start
  58.3 0.0 copy-done.2
  58.3 18.7 %reduce-scatter.3.cloned.1.call-done = bf16[32,3072]{1,0:T(8,128)(2,1)} async-done(((bf16[128,3072]{1,0:T(8,128)(2,1)}), bf16[32,3072]{1,0:T(8,128)(2,1)}) %reduce-scatter.3.cloned.1.call-update) | async-done | bytes 196624 | tf_op jit(solution)/shard_map/reduce_scatter | solution.py:66
  77.0 0.0 copy-done
  77.0 1.1 fusion.69
  78.1 1.0 fusion.71
  79.2 11.6 %all_gather.7 = bf16[128,3072]{1,0:T(8,128)(2,1)S(1)} all-gather(bf16[32,3072]{1,0:T(8,128)(2,1)S(1)} %fusion.71), channel_id=1, replica_groups=mesh['dp'=2,'tp'=4] {'tp'}, dimensions={0}, use_global_device_ids=true | all-gather | bytes 983040 | tf_op jit(solution)/shard_map/all_gather | solution.py:69
  90.8 6.4 %fusion.137 = f32[128,2048]{1,0:T(8,128)S(1)} fusion(bf16[128,3072]{1,0:T(8,128)(2,1)S(1)} %all_gather.7, bf16[3072,2048]{1,0:T(8,128)(2,1)} %param.17), kind=kOutput, calls=%fused_computation.225 | convolution fusion | flops 1610612736 | bytes 14417920 | tf_op jit(solution)/shard_map/dot_general | solution.py:70
  97.2 0.0 copy-start.1
  97.2 12.7 %convolution_convert_fusion = bf16[128,3072]{1,0:T(8,128)(2,1)} fusion(bf16[2048,3072]{1,0:T(8,128)(2,1)} %param.19, bf16[128,3072]{1,0:T(8,128)(2,1)S(1)} %all_gather.7, bf16[3072,2048]{1,0:T(8,128)(2,1)} %param.18, f32[128,2048]{1,0:T(8,128)S(1)} %fusion.137), kind=kOutput, calls=%fused_computation.10 | convolution fusion | flops 3223191552 | bytes 27787264 | tf_op jit(solution)/shard_map/dot_general | solution.py:73
  109.8 0.0 reduce-scatter.5.cloned.1.call-update
  109.9 0.7 copy.34
  110.6 0.8 copy.33
  111.3 16.0 %reduce-scatter.5.cloned.1.call-done = bf16[32,3072]{1,0:T(8,128)(2,1)} async-done(((bf16[128,3072]{1,0:T(8,128)(2,1)}), bf16[32,3072]{1,0:T(8,128)(2,1)}) %reduce-scatter.5.cloned.1.call-update) | async-done | bytes 196624 | tf_op jit(solution)/shard_map/reduce_scatter | solution.py:74
  127.3 1.7 %fusion.72 = bf16[32,3072]{1,0:T(8,128)(2,1)} fusion(bf16[32,3072]{1,0:T(8,128)(2,1)} %reduce-scatter.5.cloned.1.call-done, bf16[32,3072]{1,0:T(8,128)(2,1)S(1)} %copy-done.1, bf16[32,3072]{1,0:T(8,128)(2,1)S(1)} %copy-done), kind=kLoop, calls=%fused_computation.95 | loop fusion | flops 786432 | bytes 786432 | tf_op jit(solution)/shard_map/convert_element_type | solution.py:75
  (17 shorter events, 0.1 us)
Async XLA Ops:
  7.2 69.9 %reduce-scatter.3.cloned.1.call-start = ((), (), s32[]{:S(2)}) async-start(), calls=%async_computation.2 | async-start | bytes 983040 | tf_op jit(solution)/shard_map/reduce_scatter | solution.py:66
  54.2 4.1 %copy-start.2 = (bf16[3072]{0:T(1024)(128)(2,1)S(1)}, bf16[3072]{0:T(1024)(128)(2,1)}, u32[]{:S(2)}) copy-start(bf16[3072]{0:T(1024)(128)(2,1)} %param.12) | copy-start | bytes 18436
  54.2 22.9 %copy-start = (bf16[32,3072]{1,0:T(8,128)(2,1)S(1)}, bf16[32,3072]{1,0:T(8,128)(2,1)}, u32[]{:S(2)}) copy-start(bf16[32,3072]{1,0:T(8,128)(2,1)} %param.10) | copy-start | bytes 589828
  58.3 69.1 %reduce-scatter.5.cloned.1.call-start = ((), (), s32[]{:S(2)}) async-start(), calls=%async_computation.3 | async-start | bytes 983040 | tf_op jit(solution)/shard_map/reduce_scatter | solution.py:74
  97.2 30.2 %copy-start.1 = (bf16[32,3072]{1,0:T(8,128)(2,1)S(1)}, bf16[32,3072]{1,0:T(8,128)(2,1)}, u32[]{:S(2)}) copy-start(bf16[32,3072]{1,0:T(8,128)(2,1)} %reduce-scatter.3.cloned.1.call-done) | copy-start | bytes 589828
Sparse Core Ops, SparseCore 0:
  58.4 18.6 reduce-scatter.2
  110.0 17.2 reduce-scatter.4
where the time goes:
time: 136 us
  waiting for transfers between devices  34.7 us (26%)
  matrix products  31.3 us (23%)
  blocking collectives  24.6 us (18%)
  local copies, waits for them, and re-layouts  21.5 us (16%)
  between operations  14.3 us (11%)
  other arithmetic  9.36 us (7%)
    reduce_scatter x1, waiting for transfers between devices, local_layer(): lax.psum_scatter(attn_part, 'tp', scatter_dimension=0, tiled=True)  18.7 us
    reduce_scatter x1, waiting for transfers between devices, local_layer(): mlp_sum = lax.psum_scatter(mlp_part, 'tp', scatter_dimension=0, tiled=True)  16 us
    all_gather x1, blocking collectives, local_layer(): gathered = lax.all_gather(normed, 'tp', axis=0, tiled=True)  13 us
    dot_general x1, matrix products, local_layer(): jnp.dot(mlp_act, w_down, preferred_element_type=jnp.float32)  12.7 us
    unnamed x10, local copies, waits for them, and re-layouts  11.7 us
    all_gather x1, blocking collectives, local_layer(): gathered_mlp = lax.all_gather(normed_mlp, 'tp', axis=0, tiled=True)  11.6 us
    dot_general x1, matrix products, local_layer(): jnp.dot(gathered_mlp, w_gate, preferred_element_type=jnp.float32)  6.37 us
    dynamic_slice x1, local copies, waits for them, and re-layouts, local_layer(): key_local = lax.dynamic_slice_in_dim(w_key, first_kv, kv_local, axis=1)  5.48 us
  transfers between devices with their start and end apart: 2, of which 2 were waited for; matrix products, arithmetic and copies ran while one was open for 1% of the time, Pallas kernels for 0%

commit v1 on v0

v1 whole, which is shorter than its diff:
```python
import functools

import jax
import jax.numpy as jnp
import numpy as np
from jax import lax
from jax.experimental import pallas as pl
from jax.experimental.pallas import tpu as pltpu
from jax.sharding import PartitionSpec as P

T = 128
D = 3072
E = 128
R = 32
NH = 6
NKV = 2
F = 2048
CK = 512
NC = D // CK
EPS = 1e-5
F32 = jnp.float32
BF16 = jnp.bfloat16
MESH = pl.DeviceIdType.MESH

DIAG, PEER, CROSS, OWN = 0, 1, 2, 3


def rope_tables():
    half = E // 2
    inv_freq = (np.float32(1.0) / np.power(np.float32(500000.0), np.arange(half, dtype=np.float32) * np.float32(2.0 / E))).astype(np.float32)
    ang = np.arange(T, dtype=np.float32)[:, None] * inv_freq[None, :]
    cos = np.cos(ang.astype(np.float64)).astype(np.float32)
    sin = np.sin(ang.astype(np.float64)).astype(np.float32)
    return np.concatenate([cos, cos], 1), np.concatenate([-sin, sin], 1)


def dot(a, b):
    return lax.dot_general(a, b, (((1,), (0,)), ((), ())), preferred_element_type=F32)


def kernel(hid, an, mn, wq, wk, wv, wo, wg, wu, wd, cost, sint,
           out, kc, vc,
           hid_v, an_v, mn_v, wq_v, wk_v, wv_v, kvw, wo_v, wg_v, wu_v, wd_v, cos_v, sin_v,
           a1, a2, qkv, o_v, dsend, drecv, lsend, lrecv, ownf, crossf, mid, gacc, uacc, u_v, out_v, kc_v, vc_v,
           in_sem, wq_sem, gu_sem, wd_sem, out_sem, ag_s, ag_r, rs_s, rs_r):
    tp = lax.axis_index("tp")
    core = lax.rem(tp, 2)
    peer = tp + 1 - 2 * core
    cross = lax.rem(tp + 2, 4)
    diag = lax.rem(peer + 2, 4)
    devs = (diag, peer, cross, tp)
    rows = [pl.ds(pl.multiple_of(R * d, R), R) for d in devs]

    def start(copies):
        for cp in copies:
            cp.start()
        return copies

    small = start([pltpu.make_async_copy(s, d, in_sem.at[i]) for i, (s, d) in enumerate(
        [(hid, hid_v), (an, an_v), (mn, mn_v), (cost, cos_v), (sint, sin_v)])])
    kvc = start([pltpu.make_async_copy(wk.at[:, tp], wk_v, in_sem.at[5]),
                 pltpu.make_async_copy(wv.at[:, tp], wv_v, in_sem.at[6])])
    wqc = start([pltpu.make_async_copy(wq.at[:, pl.ds(CK * c, CK), :], wq_v.at[:, pl.ds(CK * c, CK), :], wq_sem.at[c])
                 for c in range(NC)])

    barrier = pltpu.get_barrier_semaphore()
    for d in (peer, cross):
        pl.semaphore_signal(barrier, inc=1, device_id={"tp": d}, device_id_type=MESH)
    pl.semaphore_wait(barrier, 2)

    def remote(src, dst, ss, rs, dev):
        return pltpu.make_async_remote_copy(src_ref=src, dst_ref=dst, send_sem=ss, recv_sem=rs,
                                            device_id={"tp": dev}, device_id_type=MESH)

    def ag_copies(ph, buf):
        blk = lambda c, p: buf.at[c, pl.ds(R * p, R), :]
        to_cross = [remote(blk(c, OWN), blk(c, CROSS), ag_s.at[ph, 0, c], ag_r.at[ph, 0, c], cross) for c in range(NC)]
        to_peer = [remote(blk(c, OWN), blk(c, PEER), ag_s.at[ph, 1, c], ag_r.at[ph, 1, c], peer) for c in range(NC)]
        fwd = [remote(blk(c, CROSS), blk(c, DIAG), ag_s.at[ph, 2, c], ag_r.at[ph, 2, c], peer) for c in range(NC)]
        return to_cross, to_peer, fwd

    def norm_send(x, gain_v, buf, copies):
        ss = None
        for c in range(NC):
            sq = x(c) * x(c)
            ss = sq if ss is None else ss + sq
        inv = lax.rsqrt(jnp.sum(ss, axis=-1, keepdims=True) * (1.0 / D) + EPS)
        gain = gain_v[...].astype(F32)
        to_cross, to_peer, _ = copies
        for c in range(NC):
            n = CK // 128
            g = jnp.concatenate([gain[c * n + j:c * n + j + 1, :] for j in range(n)], axis=1)
            buf[c, R * OWN:R * OWN + R, :] = (x(c) * inv * g).astype(BF16)
            to_cross[c].start()
            to_peer[c].start()

    for cp in small[:2]:
        cp.wait()
    ag1 = ag_copies(0, a1)
    norm_send(lambda c: hid_v[:, CK * c:CK * c + CK].astype(F32), an_v, a1, ag1)

    i0 = lax.broadcasted_iota(jnp.int32, (256, 256), 0)
    i1 = lax.broadcasted_iota(jnp.int32, (256, 256), 1)
    src_row = jnp.where(i0 < 128, 2 * i0, 2 * i0 - 255)
    perm = jnp.where(src_row == i1, 1.0, 0.0).astype(BF16)
    for cp in kvc:
        cp.wait()

    def split(b, _):
        dst = pl.ds(pl.multiple_of(128 * b, 128), 128)
        blk = jnp.concatenate([wk_v[dst].reshape(256, E), wv_v[dst].reshape(256, E)], axis=1)
        r = dot(perm, blk).astype(BF16)
        kvw[0, dst, :] = r[:128, :128]
        kvw[1, dst, :] = r[128:, :128]
        kvw[2, dst, :] = r[:128, 128:]
        kvw[3, dst, :] = r[128:, 128:]
        return 0

    lax.fori_loop(0, 2 * D // 256, split, 0)

    woc = pltpu.make_async_copy(wo, wo_v, in_sem.at[7])
    woc.start()
    guc = []
    for c in range(NC):
        guc.append(start([pltpu.make_async_copy(s.at[pl.ds(CK * c, CK), :], d.at[pl.ds(CK * c, CK), :], gu_sem.at[i, c])
                          for i, (s, d) in enumerate([(wg, wg_v), (wu, wu_v)])]))
    wdc = start([pltpu.make_async_copy(wd.at[pl.ds(512 * c, 512), :], wd_v.at[pl.ds(512 * c, 512), :], wd_sem.at[c])
                 for c in range(F // 512)])

    def gather_loop(copies, compute):
        to_cross, to_peer, fwd = copies
        for c in range(NC + 1):
            if c < NC:
                to_cross[c].wait_recv()
                fwd[c].start()
            if c >= 1:
                to_peer[c - 1].wait_recv()
                fwd[c - 1].wait_recv()
                compute(c - 1)
        for c in range(NC):
            to_cross[c].wait_send()
            to_peer[c].wait_send()
            fwd[c].wait_send()

    def qkv_chunk(c):
        wqc[c].wait()
        lhs = a1[c]
        for h in range(NH + 2 * NKV):
            w = wq_v[h, CK * c:CK * c + CK, :] if h < NH else kvw[h - NH, CK * c:CK * c + CK, :]
            p = dot(lhs, w)
            qkv[h] = p if c == 0 else qkv[h] + p

    gather_loop(ag1, qkv_chunk)

    for cp in small[3:]:
        cp.wait()
    cos = jnp.concatenate([cos_v[r, :] for r in rows], axis=0)
    sin = jnp.concatenate([sin_v[r, :] for r in rows], axis=0)

    def token_of(i):
        b = i // R
        base = jnp.where(b == DIAG, diag, jnp.where(b == PEER, peer, jnp.where(b == CROSS, cross, tp)))
        return base * R + i % R

    visible = (token_of(lax.broadcasted_iota(jnp.int32, (T, T), 1))
               <= token_of(lax.broadcasted_iota(jnp.int32, (T, T), 0)))

    def rope(x):
        return (x * cos + pltpu.roll(x, E // 2, 1) * sin).astype(BF16)

    for g in range(NKV):
        k = rope(qkv[NH + g])
        v = qkv[NH + NKV + g].astype(BF16)
        for p in range(4):
            kc_v[g, rows[p], :] = k[R * p:R * p + R]
            vc_v[g, rows[p], :] = v[R * p:R * p + R]
        for r in range(NH // NKV):
            h = g * (NH // NKV) + r
            q = rope(qkv[h])
            s = lax.dot_general(q, k, (((1,), (1,)), ((), ())), preferred_element_type=F32) * (E ** -0.5)
            s = jnp.where(visible, s, -1e30)
            e = jnp.exp(s - jnp.max(s, axis=-1, keepdims=True))
            pr = (e / jnp.sum(e, axis=-1, keepdims=True)).astype(BF16)
            o_v[:, E * h:E * h + E] = dot(pr, v).astype(BF16)
    cache_out = start([pltpu.make_async_copy(kc_v, kc, out_sem.at[NC]), pltpu.make_async_copy(vc_v, vc, out_sem.at[NC + 1])])

    def reduce_phase(ph, product):
        d2d = [remote(dsend.at[ph, n], drecv.at[ph, n], rs_s.at[ph, 0, n], rs_r.at[ph, 0, n], peer) for n in range(NC)]
        link = [remote(lsend.at[ph, n], lrecv.at[ph, n], rs_s.at[ph, 1, n], rs_r.at[ph, 1, n], cross) for n in range(NC)]
        for n in range(NC + 1):
            if n < NC:
                p = product(n)
                dsend[ph, n] = p[:2 * R].astype(BF16)
                crossf[n] = p[R * CROSS:R * CROSS + R]
                ownf[n] = p[R * OWN:R * OWN + R]
                d2d[n].start()
            if n >= 1:
                d2d[n - 1].wait_recv()
                lsend[ph, n - 1] = (crossf[n - 1] + drecv[ph, n - 1, :R].astype(F32)).astype(BF16)
                link[n - 1].start()
        return d2d, link

    def total(ph, n):
        return ownf[n] + drecv[ph, n, R:].astype(F32) + lrecv[ph, n].astype(F32)

    woc.wait()
    d2d, link = reduce_phase(0, lambda n: dot(o_v[...], wo_v[:, CK * n:CK * n + CK]))
    for n in range(NC):
        link[n].wait_recv()
        mid[n] = (hid_v[:, CK * n:CK * n + CK].astype(F32) + total(0, n)).astype(BF16)
    small[2].wait()
    ag2 = ag_copies(1, a2)
    norm_send(lambda c: mid[c].astype(F32), mn_v, a2, ag2)
    for n in range(NC):
        d2d[n].wait_send()
        link[n].wait_send()

    NB = 512

    def gu_chunk(c):
        for cp in guc[c]:
            cp.wait()

        def block(b, _):
            col = pl.ds(pl.multiple_of(NB * b, NB), NB)
            pg = dot(a2[c], wg_v[CK * c:CK * c + CK, col])
            pu = dot(a2[c], wu_v[CK * c:CK * c + CK, col])
            if c == 0:
                gacc[:, col] = pg
                uacc[:, col] = pu
            elif c < NC - 1:
                gacc[:, col] += pg
                uacc[:, col] += pu
            else:
                gate = gacc[:, col] + pg
                up = uacc[:, col] + pu
                u_v[:, col] = (gate * jax.nn.sigmoid(gate) * up).astype(BF16)
            return 0

        lax.fori_loop(0, F // NB, block, 0)

    gather_loop(ag2, gu_chunk)

    for cp in wdc:
        cp.wait()
    d2d, link = reduce_phase(1, lambda n: dot(u_v[...], wd_v[:, CK * n:CK * n + CK]))
    outs = []
    for n in range(NC):
        link[n].wait_recv()
        out_v[n] = (mid[n].astype(F32) + total(1, n)).astype(BF16)
        cp = pltpu.make_async_copy(out_v.at[n], out.at[:, pl.ds(CK * n, CK)], out_sem.at[n])
        cp.start()
        outs.append(cp)
    for n in range(NC):
        d2d[n].wait_send()
        link[n].wait_send()
    for cp in outs + cache_out:
        cp.wait()


def solution(mesh):
    def local_layer(hidden_in, attn_norm, mlp_norm, w_query, w_key, w_value, w_out, w_gate, w_up, w_down):
        cos, sin = rope_tables()
        any_spec = pl.BlockSpec(memory_space=pl.ANY)
        vm = pltpu.VMEM
        dma = pltpu.SemaphoreType.DMA
        out, kc, vc = pl.pallas_call(
            kernel,
            name="layer",
            out_shape=[jax.ShapeDtypeStruct((R, D), BF16),
                       jax.ShapeDtypeStruct((NKV, T, E), BF16),
                       jax.ShapeDtypeStruct((NKV, T, E), BF16)],
            in_specs=[any_spec] * 12,
            out_specs=[any_spec] * 3,
            scratch_shapes=[
                vm((R, D), BF16), vm((D // 128, 128), BF16), vm((D // 128, 128), BF16),
                vm((NH, D, E), BF16), vm((D, 2, E), BF16), vm((D, 2, E), BF16), vm((2 * NKV, D, E), BF16),
                vm((NH * E, D), BF16), vm((D, F), BF16), vm((D, F), BF16), vm((F, D), BF16),
                vm((T, E), F32), vm((T, E), F32),
                vm((NC, T, CK), BF16), vm((NC, T, CK), BF16),
                vm((NH + 2 * NKV, T, E), F32), vm((T, NH * E), BF16),
                vm((2, NC, 2 * R, CK), BF16), vm((2, NC, 2 * R, CK), BF16),
                vm((2, NC, R, CK), BF16), vm((2, NC, R, CK), BF16),
                vm((NC, R, CK), F32), vm((NC, R, CK), F32), vm((NC, R, CK), BF16),
                vm((T, F), F32), vm((T, F), F32), vm((T, F), BF16),
                vm((NC, R, CK), BF16), vm((NKV, T, E), BF16), vm((NKV, T, E), BF16),
                dma((8,)), dma((NC,)), dma((2, NC)), dma((F // 512,)), dma((NC + 2,)),
                dma((2, 3, NC)), dma((2, 3, NC)), dma((2, 2, NC)), dma((2, 2, NC)),
            ],
            compiler_params=pltpu.CompilerParams(collective_id=0, has_side_effects=True, vmem_limit_bytes=67043328),
        )(hidden_in, attn_norm.reshape(D // 128, 128), mlp_norm.reshape(D // 128, 128),
          jnp.transpose(w_query, (1, 0, 2)), w_key.reshape(D, 4, 2, E), w_value.reshape(D, 4, 2, E),
          w_out.reshape(NH * E, D), w_gate, w_up, w_down, jnp.asarray(cos), jnp.asarray(sin))
        return out, jnp.transpose(kc, (1, 0, 2)), jnp.transpose(vc, (1, 0, 2))

    row_spec = P(("dp", "tp"), None)
    cache_spec = P("dp", "tp", None)
    return jax.shard_map(local_layer, mesh=mesh, in_specs=(row_spec, P(), P(), P(None, "tp", None), P(), P(), P("tp", None, None), P(None, "tp"), P(None, "tp"), P("tp", None)), out_specs=(row_spec, cache_spec, cache_spec), check_vma=False)
```

time: 136 us -> 57.7 us (0.42)
  Pallas kernels: 0 us -> 52.1 us
  waiting for transfers between devices: 34.7 us -> 0 us
  matrix products: 31.3 us -> 0 us
  blocking collectives: 24.6 us -> 0 us
  local copies, waits for them, and re-layouts: 21.5 us -> 4.69 us
  between operations: 14.3 us -> 0.64 us
  other arithmetic: 9.36 us -> 0 us
    pallas_call x0 -> x1, Pallas kernels: none -> 52.1 us  [local_layer(): pl.pallas_call(kernel, name='layer', out_shape=[jax.ShapeDtypeStruct((R,...]
    reduce_scatter x2 -> x0, waiting for transfers between devices: 34.7 us -> none  [the longest x1 18.7 us: local_layer(): lax.psum_scatter(attn_part, 'tp', scatter_dimension=0, tiled=True)]
    dot_general x20 -> x0, matrix products: 27 us -> none  [the longest x1 12.7 us: local_layer(): jnp.dot(mlp_act, w_down, preferred_element_type=jnp.float32)]
    all_gather x2 -> x0, blocking collectives: 24.6 us -> none  [the longest x1 13 us: local_layer(): gathered = lax.all_gather(normed, 'tp', axis=0, tiled=True)]
    dynamic_slice x2 -> x0, local copies, waits for them, and re-layouts: 9.8 us -> none  [the longest x1 5.48 us: local_layer(): key_local = lax.dynamic_slice_in_dim(w_key, first_kv, kv_local, axis=1)]
    unnamed x10 -> x3, local copies, waits for them, and re-layouts: 11.7 us -> 4.69 us
    convert_element_type x6 -> x0, other arithmetic: 4.47 us -> none  [the longest x2 2.09 us: rms_norm(): (rows_f * lax.rsqrt(mean_sq + 1e-05) * gain_vec.astype(jnp.float32)).asty...]
    unnamed x2 -> x0, matrix products: 4.28 us -> none
  transfers between devices with their start and end apart: 2 -> 0, of which waited for: 2 -> 0; matrix products, arithmetic and copies ran while one was open for 1% -> 0% of each run, Pallas kernels for 0% -> 0%
where the time goes in v1:
time: 57.7 us; the launch traced here: 57.4 us
  Pallas kernels  52.1 us (90%)
  local copies, waits for them, and re-layouts  4.69 us (8%)
  between operations  0.64 us (1%)
    pallas_call x1, Pallas kernels, local_layer(): pl.pallas_call(kernel, name='layer', out_shape=[jax.ShapeDtypeStruct((R,...  52.1 us
    unnamed x3, local copies, waits for them, and re-layouts  4.69 us

profile of v1, /device:TPU:0, one launch (start us, length us, event | category | flops | bytes accessed | tf_op | source)
XLA Modules:
  0.0 57.4 jit_solution(17394689047640468912)
XLA Ops:
  0.6 52.1 %layer.1 = (bf16[32,3072]{1,0:T(8,128)(2,1)}, bf16[2,128,128]{2,1,0:T(8,128)(2,1)}, bf16[2,128,128]{2,1,0:T(8,128)(2,1)}) custom-call(bf16[32,3072]{1,0:T(8,128)(2,1)} %hid.1, bf16[24,128]{1,0:T(8,128)(2,1)} %bitcast.14, bf16[24,128]{1,0:T(8,128)(2,1)} %bitcast.15, bf16[6,3072,128]{2,1,0:T(8,128)(2,1)} %bitcast.10, bf16[3072,4,2,128]{3,2,1,0:T(2,128)(2,1)} %bitcast.8, ...), custom_call_target="tpu_custom_call" | custom-call | tf_op jit(solution)/shard_map/layer/pallas_call | solution.py:267
  52.8 1.5 %copy.15 = bf16[128,2,128]{2,1,0:T(2,128)(2,1)} copy(bf16[128,2,128]{2,0,1:T(8,128)(2,1)} %bitcast.13) | data formatting | bytes 131072
  54.3 1.5 %copy.16 = bf16[128,2,128]{2,1,0:T(2,128)(2,1)} copy(bf16[128,2,128]{2,0,1:T(8,128)(2,1)} %bitcast.12) | data formatting | bytes 131072
  55.8 1.6 %copy.18 = bf16[32,3072]{1,0:T(8,128)(2,1)} copy(bf16[32,3072]{1,0:T(8,128)(2,1)} %get-tuple-element.15) | data formatting | bytes 393216

commit v2 on v1

v2 whole, which is shorter than its diff:
```python
import functools

import jax
import jax.numpy as jnp
import numpy as np
from jax import lax
from jax.experimental import pallas as pl
from jax.experimental.pallas import tpu as pltpu
from jax.sharding import PartitionSpec as P

T = 128
D = 3072
E = 128
R = 32
NH = 6
NKV = 2
F = 2048
CK = 512
NC = D // CK
EPS = 1e-5
F32 = jnp.float32
BF16 = jnp.bfloat16
MESH = pl.DeviceIdType.MESH
scope = jax.named_scope

SUB = 256
AG1 = ((0, 1), (1, 1), (2, 2), (4, 2), (6, 2), (8, 2), (10, 1), (11, 1))
AG2 = ((0, 1), (1, 1), (2, 2), (4, 2), (6, 2), (8, 2), (10, 2))
DEPTH = 3

DIAG, CROSS, PEER, OWN = 0, 1, 2, 3


def rope_tables():
    half = E // 2
    inv_freq = (np.float32(1.0) / np.power(np.float32(500000.0), np.arange(half, dtype=np.float32) * np.float32(2.0 / E))).astype(np.float32)
    ang = np.arange(T, dtype=np.float32)[:, None] * inv_freq[None, :]
    cos = np.cos(ang.astype(np.float64)).astype(np.float32)
    sin = np.sin(ang.astype(np.float64)).astype(np.float32)
    return np.concatenate([cos, cos], 1), np.concatenate([-sin, sin], 1)


def dot(a, b):
    return lax.dot_general(a, b, (((1,), (0,)), ((), ())), preferred_element_type=F32)


def kernel(hid, an, mn, wq, wk, wv, wo, wg, wu, wd, cost, sint,
           out, kc, vc,
           hid_v, an_v, mn_v, wq_v, wk_v, wv_v, kvw, wo_v, wg_v, wu_v, wd_v, cos_v, sin_v,
           a1, a2, qkv, o_v, dsend, drecv, lsend, lrecv, ownf, crossf, mid, gacc, uacc, u_v, k_v, v_v,
           in_sem, wq_sem, gu_sem, wd_sem, ag_s, ag_r, rs_s, rs_r):
    tp = lax.axis_index("tp")
    core = lax.rem(tp, 2)
    peer = tp + 1 - 2 * core
    cross = lax.rem(tp + 2, 4)
    diag = lax.rem(peer + 2, 4)
    devs = (diag, cross, peer, tp)
    rows = [pl.ds(pl.multiple_of(R * d, R), R) for d in devs]

    def start(copies):
        for cp in copies:
            cp.start()
        return copies

    small = start([pltpu.make_async_copy(s, d, in_sem.at[i]) for i, (s, d) in enumerate(
        [(hid, hid_v), (an, an_v), (mn, mn_v), (cost, cos_v), (sint, sin_v)])])
    kvc = start([pltpu.make_async_copy(wk.at[:, tp], wk_v, in_sem.at[5]),
                 pltpu.make_async_copy(wv.at[:, tp], wv_v, in_sem.at[6])])

    barrier = pltpu.get_barrier_semaphore()
    for d in (peer, cross):
        pl.semaphore_signal(barrier, inc=1, device_id={"tp": d}, device_id_type=MESH)

    wqc = start([pltpu.make_async_copy(wq.at[:, pl.ds(SUB * a, SUB * n), :], wq_v.at[:, pl.ds(SUB * a, SUB * n), :], wq_sem.at[c])
                 for c, (a, n) in enumerate(AG1)])
    woc = pltpu.make_async_copy(wo, wo_v, in_sem.at[7])
    woc.start()
    with scope("barrier"):
        pl.semaphore_wait(barrier, 2)

    def remote(src, dst, ss, rs, dev):
        return pltpu.make_async_remote_copy(src_ref=src, dst_ref=dst, send_sem=ss, recv_sem=rs,
                                            device_id={"tp": dev}, device_id_type=MESH)

    def ag_copies(ph, buf, plan):
        def copies(i, p, q, dev):
            return [remote(buf.at[pl.ds(a, n), pl.ds(R * p, R), :], buf.at[pl.ds(a, n), pl.ds(R * q, R), :],
                           ag_s.at[ph, i, c], ag_r.at[ph, i, c], dev) for c, (a, n) in enumerate(plan)]
        return copies(0, OWN, CROSS, cross), copies(1, OWN, PEER, peer), copies(2, CROSS, DIAG, peer)

    def norm_send(x, gain_v, buf, plan, copies):
        ss = None
        for i in range(D // SUB):
            sq = x(i) * x(i)
            ss = sq if ss is None else ss + sq
        inv = lax.rsqrt(jnp.sum(ss, axis=-1, keepdims=True) * (1.0 / D) + EPS)
        gain = gain_v[...].astype(F32)
        to_cross, to_peer, _ = copies

        def send(c):
            if c < DEPTH:
                to_cross[c].start()
            to_peer[c].start()

        for c, (a, n) in enumerate(plan):
            for i in range(a, a + n):
                g = jnp.concatenate([gain[2 * i:2 * i + 1, :], gain[2 * i + 1:2 * i + 2, :]], axis=1)
                buf[i, R * OWN:R * OWN + R, :] = (x(i) * inv * g).astype(BF16)
            if c >= 1:
                send(c - 1)
        send(len(plan) - 1)

    ag1 = ag_copies(0, a1, AG1)
    with scope("hidwait"):
        for cp in small[:2]:
            cp.wait()
    with scope("norm1"):
        norm_send(lambda i: hid_v[:, SUB * i:SUB * i + SUB].astype(F32), an_v, a1, AG1, ag1)

    i0 = lax.broadcasted_iota(jnp.int32, (256, 256), 0)
    i1 = lax.broadcasted_iota(jnp.int32, (256, 256), 1)
    perm = jnp.where(jnp.where(i0 < 128, 2 * i0, 2 * i0 - 255) == i1, 1.0, 0.0).astype(BF16)
    with scope("kvwait"):
        for cp in kvc:
            cp.wait()

    def split(b, _):
        dst = pl.ds(pl.multiple_of(128 * b, 128), 128)
        blk = jnp.concatenate([wk_v[dst].reshape(256, E), wv_v[dst].reshape(256, E)], axis=1)
        r = dot(perm, blk).astype(BF16)
        kvw[0, dst, :] = r[:128, :128]
        kvw[1, dst, :] = r[128:, :128]
        kvw[2, dst, :] = r[:128, 128:]
        kvw[3, dst, :] = r[128:, 128:]
        return 0

    with scope("split"):
        lax.fori_loop(0, D // 128, split, 0, unroll=8)

    guc = []
    for c, (a, n) in enumerate(AG2):
        guc.append(start([pltpu.make_async_copy(s.at[pl.ds(SUB * a, SUB * n), :], d.at[pl.ds(SUB * a, SUB * n), :], gu_sem.at[i, c])
                          for i, (s, d) in enumerate([(wg, wg_v), (wu, wu_v)])]))
    wdc = start([pltpu.make_async_copy(wd.at[pl.ds(512 * c, 512), :], wd_v.at[pl.ds(512 * c, 512), :], wd_sem.at[c])
                 for c in range(F // 512)])

    def gather_loop(name, copies, compute):
        to_cross, to_peer, fwd = copies
        n = len(fwd)
        for c in range(n + 1):
            if c < n:
                with scope(f"{name}_x{c}"):
                    to_cross[c].wait_recv()
                fwd[c].start()
                if c + DEPTH < n:
                    with scope(f"{name}_s{c}"):
                        to_cross[c].wait_send()
                    to_cross[c + DEPTH].start()
            if c >= 1:
                with scope(f"{name}_f{c - 1}"):
                    to_peer[c - 1].wait_recv()
                    fwd[c - 1].wait_recv()
                with scope(f"{name}_c{c - 1}"):
                    compute(c - 1)
        with scope(f"{name}_ws"):
            for c in range(n):
                if c + DEPTH >= n:
                    to_cross[c].wait_send()
                to_peer[c].wait_send()
                fwd[c].wait_send()

    def lhs_of(buf, a, n):
        return buf[a] if n == 1 else jnp.concatenate([buf[a + i] for i in range(n)], axis=1)

    def qkv_chunk(c):
        a, n = AG1[c]
        wqc[c].wait()
        lhs = lhs_of(a1, a, n)
        for h in range(NH + 2 * NKV):
            w = wq_v[h, SUB * a:SUB * (a + n), :] if h < NH else kvw[h - NH, SUB * a:SUB * (a + n), :]
            p = dot(lhs, w)
            qkv[h] = p if c == 0 else qkv[h] + p

    gather_loop("ag1", ag1, qkv_chunk)

    for cp in small[3:]:
        cp.wait()
    cos = jnp.concatenate([cos_v[r, :] for r in rows], axis=0)
    sin = jnp.concatenate([sin_v[r, :] for r in rows], axis=0)

    def token_of(i):
        b = i // R
        base = jnp.where(b == DIAG, diag, jnp.where(b == CROSS, cross, jnp.where(b == PEER, peer, tp)))
        return base * R + i % R

    visible = (token_of(lax.broadcasted_iota(jnp.int32, (T, T), 1))
               <= token_of(lax.broadcasted_iota(jnp.int32, (T, T), 0)))

    def rope(x, half=None):
        cs, sn = (cos, sin) if half is None else (cos[half], sin[half])
        return (x * cs + pltpu.roll(x, E // 2, 1) * sn).astype(BF16)

    def keys_values():
        for g in range(NKV):
            k = rope(qkv[NH + g])
            v = qkv[NH + NKV + g].astype(BF16)
            for p in range(4):
                k_v[g, rows[p], :] = k[R * p:R * p + R]
                v_v[g, rows[p], :] = v[R * p:R * p + R]
            qkv[NH + g] = k.astype(F32)

    def attend(half, g):
        k = qkv[NH + g].astype(BF16)
        v = qkv[NH + NKV + g].astype(BF16)
        for r in range(NH // NKV):
            h = g * (NH // NKV) + r
            q = rope(qkv[h, half], half)
            s = lax.dot_general(q, k, (((1,), (1,)), ((), ())), preferred_element_type=F32) * (E ** -0.5)
            s = jnp.where(visible[half], s, -1e30)
            e = jnp.exp(s - jnp.max(s, axis=-1, keepdims=True))
            pr = (e * (1.0 / jnp.sum(e, axis=-1, keepdims=True))).astype(BF16)
            o_v[half, E * h:E * h + E] = dot(pr, v).astype(BF16)

    far, near = slice(0, 2 * R), slice(2 * R, 4 * R)

    def rs_copies(ph):
        row = lambda buf, n, i: buf.at[ph, n, pl.ds(R * i, R), :]
        dfar = [remote(row(dsend, n, 0), row(drecv, n, 0), rs_s.at[ph, 0, n], rs_r.at[ph, 0, n], peer) for n in range(NC)]
        dnear = [remote(row(dsend, n, 1), row(drecv, n, 1), rs_s.at[ph, 1, n], rs_r.at[ph, 1, n], peer) for n in range(NC)]
        link = [remote(lsend.at[ph, n], lrecv.at[ph, n], rs_s.at[ph, 2, n], rs_r.at[ph, 2, n], cross) for n in range(NC)]
        return dfar, dnear, link

    def send_sum(ph, copies, n):
        dfar, _, link = copies
        with scope(f"rs{ph}_d{n}"):
            dfar[n].wait_recv()
        lsend[ph, n] = (crossf[n] + drecv[ph, n, :R].astype(F32)).astype(BF16)
        link[n].start()

    def put_far(ph, copies, n, p):
        dsend[ph, n, :R] = p[:R].astype(BF16)
        crossf[n] = p[R:2 * R]
        copies[0][n].start()

    def put_near(ph, copies, n, p):
        dsend[ph, n, R:] = p[:R].astype(BF16)
        ownf[n] = p[R:2 * R]
        copies[1][n].start()

    def total(ph, copies, n):
        with scope(f"rs{ph}_n{n}"):
            copies[1][n].wait_recv()
        part = ownf[n] + drecv[ph, n, R:].astype(F32)
        with scope(f"rs{ph}_x{n}"):
            copies[2][n].wait_recv()
        return part + lrecv[ph, n].astype(F32)

    def drain(copies):
        for group in copies:
            for cp in group:
                cp.wait_send()

    rs0 = rs_copies(0)
    with scope("attnA"):
        keys_values()
        for g in range(NKV):
            attend(far, g)
    with scope("wowait"):
        woc.wait()
    for n in range(NC):
        with scope(f"rs0_p{n}"):
            put_far(0, rs0, n, dot(o_v[far, :], wo_v[:, CK * n:CK * n + CK]))
        if n >= 4:
            send_sum(0, rs0, n - 4)
    with scope("attnB0"):
        attend(near, 0)
    send_sum(0, rs0, 2)
    send_sum(0, rs0, 3)
    with scope("attnB1"):
        attend(near, 1)
    send_sum(0, rs0, 4)
    send_sum(0, rs0, 5)
    for n in range(NC):
        with scope(f"rs0_q{n}"):
            put_near(0, rs0, n, dot(o_v[near, :], wo_v[:, CK * n:CK * n + CK]))

    with scope("cache"):
        inter = jnp.where(i1 == i0 // 2 + 128 * (i0 % 2), 1.0, 0.0).astype(BF16)
        kv = jnp.concatenate([jnp.concatenate([k_v[0], k_v[1]], axis=0), jnp.concatenate([v_v[0], v_v[1]], axis=0)], axis=1)
        kv = dot(inter, kv).astype(BF16)
        kc[...] = kv[:, :E]
        vc[...] = kv[:, E:]

    for n in range(NC):
        t = total(0, rs0, n)
        m = (hid_v[:, CK * n:CK * n + CK].astype(F32) + t).astype(BF16)
        mid[2 * n] = m[:, :SUB]
        mid[2 * n + 1] = m[:, SUB:]
    small[2].wait()
    ag2 = ag_copies(1, a2, AG2)
    with scope("norm2"):
        norm_send(lambda i: mid[i].astype(F32), mn_v, a2, AG2, ag2)
    drain(rs0)

    NB = 512

    def gu_chunk(c):
        a, n = AG2[c]
        for cp in guc[c]:
            cp.wait()
        lhs = lhs_of(a2, a, n)
        k = slice(SUB * a, SUB * (a + n))
        for b in range(F // NB):
            col = slice(NB * b, NB * b + NB)
            pg = dot(lhs, wg_v[k, col])
            pu = dot(lhs, wu_v[k, col])
            if c == 0:
                gacc[:, col] = pg
                uacc[:, col] = pu
            elif c < len(AG2) - 1:
                gacc[:, col] += pg
                uacc[:, col] += pu
            else:
                gate = gacc[:, col] + pg
                up = uacc[:, col] + pu
                u_v[:, col] = (gate * jax.nn.sigmoid(gate) * up).astype(BF16)

    gather_loop("ag2", ag2, gu_chunk)

    with scope("wdwait"):
        for cp in wdc:
            cp.wait()
    rs1 = rs_copies(1)
    LA = 2
    for n in range(NC + LA):
        if n < NC:
            with scope(f"rs1_p{n}"):
                p = dot(u_v[...], wd_v[:, CK * n:CK * n + CK])
                put_far(1, rs1, n, p[far])
                put_near(1, rs1, n, p[near])
        if n >= LA:
            send_sum(1, rs1, n - LA)
    for n in range(NC):
        t = total(1, rs1, n)
        m = jnp.concatenate([mid[2 * n], mid[2 * n + 1]], axis=1).astype(F32)
        out[:, CK * n:CK * n + CK] = (m + t).astype(BF16)
    drain(rs1)


def store_kernel(a, b, c, oa, ob, oc, sem):
    copies = [pltpu.make_async_copy(s, d, sem.at[i]) for i, (s, d) in enumerate([(a, oa), (b, ob), (c, oc)])]
    for cp in copies:
        cp.start()
    for cp in copies:
        cp.wait()


def solution(mesh):
    def local_layer(hidden_in, attn_norm, mlp_norm, w_query, w_key, w_value, w_out, w_gate, w_up, w_down):
        cos, sin = rope_tables()
        any_spec = pl.BlockSpec(memory_space=pl.ANY)
        vm = pltpu.VMEM
        dma = pltpu.SemaphoreType.DMA
        vm_spec = pl.BlockSpec(memory_space=pltpu.VMEM)
        shapes = [(R, D), (NKV * T, E), (NKV * T, E)]
        res = pl.pallas_call(
            kernel,
            name="layer",
            out_shape=[vm(s, BF16) for s in shapes],
            in_specs=[any_spec] * 12,
            out_specs=[vm_spec] * 3,
            scratch_shapes=[
                vm((R, D), BF16), vm((D // 128, 128), BF16), vm((D // 128, 128), BF16),
                vm((NH, D, E), BF16), vm((D, 2, E), BF16), vm((D, 2, E), BF16), vm((2 * NKV, D, E), BF16),
                vm((NH * E, D), BF16), vm((D, F), BF16), vm((D, F), BF16), vm((F, D), BF16),
                vm((T, E), F32), vm((T, E), F32),
                vm((D // SUB, T, SUB), BF16), vm((D // SUB, T, SUB), BF16),
                vm((NH + 2 * NKV, T, E), F32), vm((T, NH * E), BF16),
                vm((2, NC, 2 * R, CK), BF16), vm((2, NC, 2 * R, CK), BF16),
                vm((2, NC, R, CK), BF16), vm((2, NC, R, CK), BF16),
                vm((NC, R, CK), F32), vm((NC, R, CK), F32), vm((D // SUB, R, SUB), BF16),
                vm((T, F), F32), vm((T, F), F32), vm((T, F), BF16),
                vm((NKV, T, E), BF16), vm((NKV, T, E), BF16),
                dma((8,)), dma((len(AG1),)), dma((2, len(AG2))), dma((F // 512,)),
                dma((2, 3, len(AG1))), dma((2, 3, len(AG1))), dma((2, 3, NC)), dma((2, 3, NC)),
            ],
            compiler_params=pltpu.CompilerParams(collective_id=0, has_side_effects=True, vmem_limit_bytes=64500000),
        )(hidden_in, attn_norm.reshape(D // 128, 128), mlp_norm.reshape(D // 128, 128),
          jnp.transpose(w_query, (1, 0, 2)), w_key.reshape(D, 4, 2, E), w_value.reshape(D, 4, 2, E),
          w_out.reshape(NH * E, D), w_gate, w_up, w_down, jnp.asarray(cos), jnp.asarray(sin))
        out, kc, vc = pl.pallas_call(
            store_kernel,
            name="store",
            out_shape=[jax.ShapeDtypeStruct(s, BF16) for s in shapes],
            in_specs=[vm_spec] * 3,
            out_specs=[any_spec] * 3,
            scratch_shapes=[dma((3,))],
            compiler_params=pltpu.CompilerParams(vmem_limit_bytes=1 << 20),
        )(*res)
        return out, kc.reshape(T, NKV, E), vc.reshape(T, NKV, E)

    row_spec = P(("dp", "tp"), None)
    cache_spec = P("dp", "tp", None)
    return jax.shard_map(local_layer, mesh=mesh, in_specs=(row_spec, P(), P(), P(None, "tp", None), P(), P(), P("tp", None, None), P(None, "tp"), P(None, "tp"), P("tp", None)), out_specs=(row_spec, cache_spec, cache_spec), check_vma=False)
```

time: 57.7 us -> 45.5 us (0.79)
  Pallas kernels: 52.1 us -> 44.8 us
  local copies, waits for them, and re-layouts: 4.69 us -> 0 us
    pallas_call x1 -> x2, Pallas kernels: 52.1 us -> 44.8 us  [the longest x1 44.1 us: local_layer(): pl.pallas_call(kernel, name='layer', out_shape=[vm(s, BF16) for s in shap...]
    unnamed x3 -> x0, local copies, waits for them, and re-layouts: 4.69 us -> none
where the time goes in v2:
time: 45.5 us; the launch traced here: 45.4 us
  Pallas kernels  44.8 us (98%)
  between operations  0.64 us (1%)
    pallas_call x1, Pallas kernels, local_layer(): pl.pallas_call(kernel, name='layer', out_shape=[vm(s, BF16) for s in shap...  44.1 us

profile of v2, /device:TPU:0, one launch (start us, length us, event | category | flops | bytes accessed | tf_op | source)
XLA Modules:
  0.0 45.4 jit_solution(11827729555189328228)
XLA Ops:
  0.6 44.1 %layer.1 = (bf16[32,3072]{1,0:T(8,128)(2,1)S(1)}, bf16[256,128]{1,0:T(8,128)(2,1)S(1)}, bf16[256,128]{1,0:T(8,128)(2,1)S(1)}) custom-call(bf16[32,3072]{1,0:T(8,128)(2,1)} %hid.1, bf16[24,128]{1,0:T(8,128)(2,1)} %bitcast.12, bf16[24,128]{1,0:T(8,128)(2,1)} %bitcast.13, bf16[6,3072,128]{2,1,0:T(8,128)(2,1)} %bitcast.10, bf16[3072,4,2,128]{3,2,1,0:T(2,128)(2,1)} %bitcast.8, ...), custom_call_target="tpu_custom_call" | custom-call | tf_op jit(solution)/shard_map/layer/pallas_call | solution.py:366
  44.7 0.7 %store.1 = (bf16[32,3072]{1,0:T(8,128)(2,1)}, bf16[256,128]{1,0:T(8,128)(2,1)}, bf16[256,128]{1,0:T(8,128)(2,1)}) custom-call(bf16[32,3072]{1,0:T(8,128)(2,1)S(1)} %get-tuple-element.9.a, bf16[256,128]{1,0:T(8,128)(2,1)S(1)} %get-tuple-element.10.b, bf16[256,128]{1,0:T(8,128)(2,1)S(1)} %get-tuple-element.11.c), custom_call_target="tpu_custom_call" | custom-call | tf_op jit(solution)/shard_map/store/pallas_call | solution.py:391
